TPU v7x, 256 devices: a 4x2x16 block of a 4x16x16 slice. The times are simulated.
256 devices in a mesh: scene: 2 (over y), cam: 128 (over x, z, core).
Axes of the slice: x: 4, y: 2, z: 16, core: 2. Of those that a mesh axis runs over, the one named last changes fastest.
The devices are a block of a 4x16x16 slice.
Arguments:
- queries: bfloat16 [256, 768, 1024], P(('scene', 'cam')), parts along dimension 0, may hold values from -32 to 32
- keys: bfloat16 [256, 768, 1024], P(('scene', 'cam')), parts along dimension 0, may hold values from -32 to 32
- values: bfloat16 [256, 768, 1024], P(('scene', 'cam')), parts along dimension 0, may hold values from -6 to 6
- residual: bfloat16 [256, 768, 1024], P(('scene', 'cam')), parts along dimension 0, may hold values from -1.5 to 1.5
- w_out: bfloat16 [1024, 1024], replicated, may hold values from -0.1875 to 0.1875
- neighbours: int32 [256, 4], P(('scene', 'cam')), parts along dimension 0, may hold values from 0 to 127, as said below
- band_start: int32 [256, 4], P(('scene', 'cam')), parts along dimension 0, may hold values from 0 to 3
- band_blocks: int32 [256, 4, 6, 2], P(('scene', 'cam')), parts along dimension 0, may hold values from 0 to 2, as said below
- band_count: int32 [256, 4, 6], P(('scene', 'cam')), parts along dimension 0, may hold values from 1 to 2, as said below
Outputs:
- output: bfloat16 [256, 768, 1024], P(('scene', 'cam')), parts along dimension 0
There are 2 independent parts, one for each index of `scene`. A program takes and returns all parts, laid end to end along the dimension named above; an argument that names none is the same for every part. Nothing has to cross between parts.
Inputs may be any that keep to these rules, and one draw needn't show every extreme that they name: `neighbours`: row v lists the views (v + k * 4) mod 128 for k = 1, -1, 2, -2, each once, in an order drawn for each row. `band_blocks`: each list holds 2 different numbers; entries at positions band_count or later are not read. `band_count`: query block 0 of every slot has 2.
All inputs are finite; a program needn't handle non-finite values.
Results may differ from a plain program's by a relative error of at most 0.008.
Values may be sent and summed in bfloat16 or wider, within the bound.
No kernel may reach another device: no remote copies, remote signals or barrier semaphores. Data moves between devices by JAX's collectives and lax.ppermute only.
A program may use at most 128 MiB of HBM per device.

v0:
```python
import math

import jax
import jax.numpy as jnp
from jax import lax
from jax.sharding import PartitionSpec as P

HEADS = 16


def passed_along(block, axis, distance):
    devices = range(lax.axis_size(axis))
    route = [((i - distance) % len(devices), i) for i in devices]
    return lax.ppermute(block, axis, route)


def shortened(x):

    def short(part):
        return part.astype(jnp.bfloat16) if part.dtype == jnp.float32 else part

    return jax.tree.map(short, x)


def per_device(
    queries, keys, values, residual, w_out, neighbours, band_start, band_blocks, band_count
):
    query_rows = queries[0]
    key_rows = keys[0]
    value_rows = values[0]
    tokens, model_width = query_rows.shape
    qblocks = band_count.shape[2]
    most_blocks = band_blocks.shape[3]
    block_len = tokens // qblocks
    window_blocks = max(2, qblocks // 2)
    head_dim = model_width // HEADS
    score_scale = 1.0 / math.sqrt(head_dim)
    cameras = lax.axis_size("cam")
    rig_count = cameras // min(32, cameras)
    self_index = lax.axis_index("cam")
    offsets = (1, -1, 2, -2)

    def cycle_of(offset):
        return (self_index + offset * rig_count + 2 * cameras) % cameras

    source_cams = jnp.stack([cycle_of(-offset) for offset in offsets])
    slot_match = (neighbours[0][None, :] == source_cams[:, None]).astype(jnp.int32)
    slot_starts = jnp.sum(slot_match * band_start[0][None, :], axis=1)
    relative = jnp.sum(slot_match[:, :, None, None] * band_blocks[0][None], axis=1)
    slot_count = jnp.sum(slot_match[:, :, None] * band_count[0][None], axis=1)

    def asked_start(position):
        offset = offsets[position]
        wanted = lax.dynamic_slice_in_dim(slot_starts, position, 1, 0)
        return passed_along(wanted, "cam", -offset * rig_count)

    def band_slice(position):
        first_block = asked_start(position)[0]
        return (
            lax.dynamic_slice_in_dim(
                key_rows, first_block * block_len, window_blocks * block_len, 0
            ),
            lax.dynamic_slice_in_dim(
                value_rows, first_block * block_len, window_blocks * block_len, 0
            ),
        )

    near_prev = passed_along(shortened(band_slice(0)), "cam", rig_count)
    near_next = passed_along(shortened(band_slice(1)), "cam", -rig_count)
    far_prev = passed_along(shortened(band_slice(2)), "cam", 2 * rig_count)
    far_next = passed_along(shortened(band_slice(3)), "cam", -2 * rig_count)
    received = (near_prev, near_next, far_prev, far_next)
    key_tiles = [buffer[0].reshape(-1, block_len, model_width) for buffer in received]
    value_tiles = [buffer[1].reshape(-1, block_len, model_width) for buffer in received]
    own_queries = query_rows.reshape(qblocks, block_len, HEADS, head_dim)
    own_keys = key_rows.reshape(qblocks, block_len, model_width)
    own_values = value_rows.reshape(qblocks, block_len, model_width)
    group_size = math.gcd(qblocks, max(1, 512 // block_len))
    group_count = qblocks // group_size

    def one_group(turn_index):
        first_block = turn_index * group_size
        query_group = lax.dynamic_slice_in_dim(own_queries, first_block, group_size, 0)
        key_parts = [lax.dynamic_slice_in_dim(own_keys, first_block, group_size, 0)]
        value_parts = [lax.dynamic_slice_in_dim(own_values, first_block, group_size, 0)]
        mask_parts = [jnp.ones((group_size, block_len), dtype=bool)]
        for source in range(4):
            block_index = lax.dynamic_slice_in_dim(relative[source], first_block, group_size, 0)
            key_parts.append(
                key_tiles[source][block_index].reshape(
                    group_size, most_blocks * block_len, model_width
                )
            )
            value_parts.append(
                value_tiles[source][block_index].reshape(
                    group_size, most_blocks * block_len, model_width
                )
            )
            live_count = lax.dynamic_slice_in_dim(slot_count[source], first_block, group_size, 0)
            live_slots = jnp.arange(most_blocks, dtype=jnp.int32)[None, :] < live_count[:, None]
            mask_parts.append(jnp.repeat(live_slots, block_len, axis=1))
        key_group = jnp.concatenate(key_parts, axis=1).reshape(group_size, -1, HEADS, head_dim)
        value_group = jnp.concatenate(value_parts, axis=1).reshape(group_size, -1, HEADS, head_dim)
        visible = jnp.concatenate(mask_parts, axis=1)
        scores = (
            jnp.einsum(
                "gqhd,gkhd->ghqk", query_group, key_group, preferred_element_type=jnp.float32
            )
            * score_scale
        )
        scores = jnp.where(visible[:, None, None, :], scores, -jnp.inf)
        row_max = jnp.max(scores, axis=-1, keepdims=True)
        expo_scores = jnp.exp(scores - row_max)
        weights = (expo_scores / jnp.sum(expo_scores, axis=-1, keepdims=True)).astype(jnp.bfloat16)
        mixed_rows = jnp.einsum(
            "ghqk,gkhd->gqhd", weights, value_group, preferred_element_type=jnp.float32
        )
        return mixed_rows.astype(jnp.bfloat16).reshape(group_size * block_len, model_width)

    attended = lax.map(one_group, jnp.arange(group_count, dtype=jnp.int32)).reshape(
        tokens, model_width
    )
    result_rows = residual[0].astype(jnp.float32) + jnp.dot(
        attended, w_out, preferred_element_type=jnp.float32
    )
    return result_rows.astype(jnp.bfloat16)[None]


def solution(mesh):
    return jax.shard_map(
        per_device,
        mesh=mesh,
        in_specs=(
            P(("scene", "cam"), None, None),
            P(("scene", "cam"), None, None),
            P(("scene", "cam"), None, None),
            P(("scene", "cam"), None, None),
            P(),
            P(("scene", "cam"), None),
            P(("scene", "cam"), None),
            P(("scene", "cam"), None, None, None),
            P(("scene", "cam"), None, None),
        ),
        out_specs=P(("scene", "cam"), None, None),
        check_vma=False,
    )
```

profile of v0, /device:TPU:40, one launch (start us, length us, event | category | flops | bytes accessed | tf_op | source)
XLA Modules:
  0.0 662.5 jit_solution(12759696888235144906)
XLA Ops:
  1.7 10.6 %collective-permute-start.6 = (s32[1]{0:T(128)}, s32[1]{0:T(128)}, u32[]{:S(2)}, u32[]{:S(2)}) collective-permute-start(s32[1]{0:T(128)} %get-tuple-element.196), channel_id=1, source_target_pairs={{120,0},{121,1},{122,2},{123,3},{124,4},{125,5},{126,6},{127,7},{0... | collective-permute-start | bytes 20 | tf_op jit(solution)/shard_map/ppermute | solution.py:14
  12.3 13.1 %collective-permute-start.4 = (s32[1]{0:T(128)}, s32[1]{0:T(128)}, u32[]{:S(2)}, u32[]{:S(2)}) collective-permute-start(s32[1]{0:T(128)} %get-tuple-element.197), channel_id=1, source_target_pairs={{8,0},{9,1},{10,2},{11,3},{12,4},{13,5},{14,6},{15,7},{16,8},{17,9... | collective-permute-start | bytes 20 | tf_op jit(solution)/shard_map/ppermute | solution.py:14
  37.4 5.0 collective-permute-start.11
  51.1 4.5 collective-permute-start.7
  55.6 58.3 %collective-permute-done.11 = bf16[384,1024]{1,0:T(8,128)(2,1)} collective-permute-done((bf16[384,1024]{1,0:T(8,128)(2,1)S(1)}, bf16[384,1024]{1,0:T(8,128)(2,1)}, u32[]{:S(2)}, u32[]{:S(2)}) %collective-permute-start.11) | collective-permute-done | bytes 786464 | tf_op jit(solution)/shard_map/ppermute | solution.py:14
  113.9 12.0 %collective-permute-start.3 = (bf16[384,1024]{1,0:T(8,128)(2,1)}, bf16[384,1024]{1,0:T(8,128)(2,1)}, u32[]{:S(2)}, u32[]{:S(2)}) collective-permute-start(bf16[384,1024]{1,0:T(8,128)(2,1)} %get-tuple-element.193), channel_id=1, source_target_pairs={{4,0},{5,1},{6,2},{7,3},{8,4},{9,5},{10,6},{11,7},{12,8},{13,9},{1... | collective-permute-start | bytes 2359304 | tf_op jit(solution)/shard_map/ppermute | solution.py:14
  125.8 30.9 %collective-permute-done.9 = bf16[384,1024]{1,0:T(8,128)(2,1)} collective-permute-done((bf16[384,1024]{1,0:T(8,128)(2,1)S(1)}, bf16[384,1024]{1,0:T(8,128)(2,1)}, u32[]{:S(2)}, u32[]{:S(2)}) %collective-permute-start.9) | collective-permute-done | bytes 786464 | tf_op jit(solution)/shard_map/ppermute | solution.py:14
  157.4 5.2 reshape.376
  162.7 4.9 copy.80
  167.7 34.2 %collective-permute-done.7 = bf16[384,1024]{1,0:T(8,128)(2,1)} collective-permute-done((bf16[384,1024]{1,0:T(8,128)(2,1)}, bf16[384,1024]{1,0:T(8,128)(2,1)}, u32[]{:S(2)}, u32[]{:S(2)}) %collective-permute-start.7) | collective-permute-done | bytes 786464 | tf_op jit(solution)/shard_map/ppermute | solution.py:14
  201.9 45.6 %collective-permute-done.3 = bf16[384,1024]{1,0:T(8,128)(2,1)} collective-permute-done((bf16[384,1024]{1,0:T(8,128)(2,1)}, bf16[384,1024]{1,0:T(8,128)(2,1)}, u32[]{:S(2)}, u32[]{:S(2)}) %collective-permute-start.3) | collective-permute-done | bytes 786464 | tf_op jit(solution)/shard_map/ppermute | solution.py:14
  247.5 13.6 %collective-permute-done.5 = bf16[384,1024]{1,0:T(8,128)(2,1)} collective-permute-done((bf16[384,1024]{1,0:T(8,128)(2,1)}, bf16[384,1024]{1,0:T(8,128)(2,1)}, u32[]{:S(2)}, u32[]{:S(2)}) %collective-permute-start.5) | collective-permute-done | bytes 786464 | tf_op jit(solution)/shard_map/ppermute | solution.py:14
  261.1 396.3 %while.10 = (s32[]{:T(128)}, bf16[3,256,1024]{2,1,0:T(8,128)(2,1)}, s32[3]{0:T(128)S(1)}, bf16[6,128,1024]{2,1,0:T(8,128)(2,1)}, s32[4,6,2]{2,1,0:T(8,128)S(1)},...) while((s32[]{:T(128)}, bf16[3,256,1024]{2,1,0:T(8,128)(2,1)}, ...), condition=%wide.region_6.7_spmd, body=%wide.region_3.6_spmd.sunk | while | flops 1236538624 | bytes 166787424 | solution.py:120
  289.4 4.0 reshape.431
  310.0 4.0 reshape.432
  375.2 11.2 %fusion.58 = (f32[2,16,128]{2,1,0:T(8,128)S(1)}, f32[2,16,128,1152]{3,2,1,0:T(8,128)}) fusion(pred[2,1152]{1,0:T(4,128)(4,1)S(1)} %constant_dynamic-update-slice_fusion.41, bf16[2,1152,16,64]{1,3,2,0:T(8,128)(2,1)} %copy-done.8, bf16[6,128,16,64]{1,3,2,0:T(8,128)(2,1)} %get-tuple-element.387, s32[]{:T(128)S(6)} %select_n.121), kind=kOutput, calls=%fused_computation.97.clone.1 | convolution fusion | flops 622855296 | bytes 24135940 | tf_op jit(solution)/shard_map/while/body/eval_jaxpr/sub | solution.py:113
  386.4 12.4 %fusion.59 = bf16[2,128,16,64]{1,3,2,0:T(8,128)(2,1)} fusion(bf16[2,1152,16,64]{1,3,2,0:T(8,128)(2,1)} %constant_dynamic-update-slice_fusion.36, f32[2,16,128,1152]{3,2,1,0:T(8,128)} %get-tuple-element.335, f32[2,16,128]{2,1,0:T(8,128)S(1)} %get-tuple-element.336), kind=kOutput, calls=%fused_computation.19.clone.1 | convolution fusion | flops 613679104 | bytes 24133632 | tf_op jit(solution)/shard_map/while/body/eval_jaxpr/ghqk,gkhd->gqhd/dot_general | solution.py:115
  416.0 4.0 reshape.431
  501.9 11.2 %fusion.58 = (f32[2,16,128]{2,1,0:T(8,128)S(1)}, f32[2,16,128,1152]{3,2,1,0:T(8,128)}) fusion(pred[2,1152]{1,0:T(4,128)(4,1)S(1)} %constant_dynamic-update-slice_fusion.41, bf16[2,1152,16,64]{1,3,2,0:T(8,128)(2,1)} %copy-done.8, bf16[6,128,16,64]{1,3,2,0:T(8,128)(2,1)} %get-tuple-element.387, s32[]{:T(128)S(6)} %select_n.121), kind=kOutput, calls=%fused_computation.97.clone.1 | convolution fusion | flops 622855296 | bytes 24135940 | tf_op jit(solution)/shard_map/while/body/eval_jaxpr/sub | solution.py:113
  513.0 12.4 %fusion.59 = bf16[2,128,16,64]{1,3,2,0:T(8,128)(2,1)} fusion(bf16[2,1152,16,64]{1,3,2,0:T(8,128)(2,1)} %constant_dynamic-update-slice_fusion.36, f32[2,16,128,1152]{3,2,1,0:T(8,128)} %get-tuple-element.335, f32[2,16,128]{2,1,0:T(8,128)S(1)} %get-tuple-element.336), kind=kOutput, calls=%fused_computation.19.clone.1 | convolution fusion | flops 613679104 | bytes 24133632 | tf_op jit(solution)/shard_map/while/body/eval_jaxpr/ghqk,gkhd->gqhd/dot_general | solution.py:115
  542.7 4.0 reshape.431
  628.5 11.2 %fusion.58 = (f32[2,16,128]{2,1,0:T(8,128)S(1)}, f32[2,16,128,1152]{3,2,1,0:T(8,128)}) fusion(pred[2,1152]{1,0:T(4,128)(4,1)S(1)} %constant_dynamic-update-slice_fusion.41, bf16[2,1152,16,64]{1,3,2,0:T(8,128)(2,1)} %copy-done.8, bf16[6,128,16,64]{1,3,2,0:T(8,128)(2,1)} %get-tuple-element.387, s32[]{:T(128)S(6)} %select_n.121), kind=kOutput, calls=%fused_computation.97.clone.1 | convolution fusion | flops 622855296 | bytes 24135940 | tf_op jit(solution)/shard_map/while/body/eval_jaxpr/sub | solution.py:113
  639.7 12.4 %fusion.59 = bf16[2,128,16,64]{1,3,2,0:T(8,128)(2,1)} fusion(bf16[2,1152,16,64]{1,3,2,0:T(8,128)(2,1)} %constant_dynamic-update-slice_fusion.36, f32[2,16,128,1152]{3,2,1,0:T(8,128)} %get-tuple-element.335, f32[2,16,128]{2,1,0:T(8,128)S(1)} %get-tuple-element.336), kind=kOutput, calls=%fused_computation.19.clone.1 | convolution fusion | flops 613679104 | bytes 24133632 | tf_op jit(solution)/shard_map/while/body/eval_jaxpr/ghqk,gkhd->gqhd/dot_general | solution.py:115
  657.3 4.8 fusion.30
  (278 shorter events, 311.3 us)
Async XLA Ops:
  0.0 657.3 %copy-start = (bf16[1024,1024]{1,0:T(8,128)(2,1)S(1)}, bf16[1024,1024]{1,0:T(8,128)(2,1)}, u32[]{:S(2)}) copy-start(bf16[1024,1024]{1,0:T(8,128)(2,1)} %param.15) | copy-start | bytes 6291460
  1.7 30.5 %collective-permute-start.6 = (s32[1]{0:T(128)}, s32[1]{0:T(128)}, u32[]{:S(2)}, u32[]{:S(2)}) collective-permute-start(s32[1]{0:T(128)} %get-tuple-element.196), channel_id=1, source_target_pairs={{120,0},{121,1},{122,2},{123,3},{124,4},{125,5},{126,6},{127,7},{0... | collective-permute-start | bytes 20 | tf_op jit(solution)/shard_map/ppermute | solution.py:14
  12.3 20.6 %collective-permute-start.4 = (s32[1]{0:T(128)}, s32[1]{0:T(128)}, u32[]{:S(2)}, u32[]{:S(2)}) collective-permute-start(s32[1]{0:T(128)} %get-tuple-element.197), channel_id=1, source_target_pairs={{8,0},{9,1},{10,2},{11,3},{12,4},{13,5},{14,6},{15,7},{16,8},{17,9... | collective-permute-start | bytes 20 | tf_op jit(solution)/shard_map/ppermute | solution.py:14
  25.4 8.3 %collective-permute-start.2 = (s32[1]{0:T(128)}, s32[1]{0:T(128)}, u32[]{:S(2)}, u32[]{:S(2)}) collective-permute-start(s32[1]{0:T(128)} %get-tuple-element.198), channel_id=1, source_target_pairs={{124,0},{125,1},{126,2},{127,3},{0,4},{1,5},{2,6},{3,7},{4,8},{5,9... | collective-permute-start | bytes 20 | tf_op jit(solution)/shard_map/ppermute | solution.py:14
  28.6 5.8 collective-permute-start
  35.1 14.3 %copy-start.7 = (bf16[1,768,1024]{2,1,0:T(8,128)(2,1)S(1)}, bf16[1,768,1024]{2,1,0:T(8,128)(2,1)}, u32[]{:S(2)}) copy-start(bf16[1,768,1024]{2,1,0:T(8,128)(2,1)} %param.13) | copy-start | bytes 4718596
  37.4 119.7 %copy-start.9 = (s32[1,4,6,2]{2,3,1,0:T(2,128)S(1)}, s32[1,4,6,2]{2,3,1,0:T(2,128)}, u32[]{:S(2)}) copy-start(s32[1,4,6,2]{2,3,1,0:T(2,128)} %param.18) | copy-start | bytes 580
  37.4 119.7 %copy-start.11 = (s32[1,4]{1,0:T(1,128)S(1)}, s32[1,4]{1,0:T(1,128)}, u32[]{:S(2)}) copy-start(s32[1,4]{1,0:T(1,128)} %param.16) | copy-start | bytes 52
  37.4 76.4 %collective-permute-start.11 = (bf16[384,1024]{1,0:T(8,128)(2,1)S(1)}, bf16[384,1024]{1,0:T(8,128)(2,1)}, u32[]{:S(2)}, u32[]{:S(2)}) collective-permute-start(bf16[384,1024]{1,0:T(8,128)(2,1)S(1)} %get-tuple-element.188), channel_id=1, source_target_pairs={{8,0},{9,1},{10,2},{11,3},{12,4},{13,5},{14,6},{15,7},{16,8},{17,9... | collective-permute-start | bytes 2359304 | tf_op jit(solution)/shard_map/ppermute | solution.py:14
  42.5 114.2 %collective-permute-start.9 = (bf16[384,1024]{1,0:T(8,128)(2,1)S(1)}, bf16[384,1024]{1,0:T(8,128)(2,1)}, u32[]{:S(2)}, u32[]{:S(2)}) collective-permute-start(bf16[384,1024]{1,0:T(8,128)(2,1)S(1)} %get-tuple-element.189), channel_id=1, source_target_pairs={{4,0},{5,1},{6,2},{7,3},{8,4},{9,5},{10,6},{11,7},{12,8},{13,9},{1... | collective-permute-start | bytes 2359304 | tf_op jit(solution)/shard_map/ppermute | solution.py:14
  44.6 112.1 %collective-permute-start.8 = (bf16[384,1024]{1,0:T(8,128)(2,1)S(1)}, bf16[384,1024]{1,0:T(8,128)(2,1)}, u32[]{:S(2)}, u32[]{:S(2)}) collective-permute-start(bf16[384,1024]{1,0:T(8,128)(2,1)S(1)} %get-tuple-element.190), channel_id=1, source_target_pairs={{124,0},{125,1},{126,2},{127,3},{0,4},{1,5},{2,6},{3,7},{4,8},{5,9... | collective-permute-start | bytes 2359304 | tf_op jit(solution)/shard_map/ppermute | solution.py:14
  45.8 121.9 %collective-permute-start.10 = (bf16[384,1024]{1,0:T(8,128)(2,1)S(1)}, bf16[384,1024]{1,0:T(8,128)(2,1)}, u32[]{:S(2)}, u32[]{:S(2)}) collective-permute-start(bf16[384,1024]{1,0:T(8,128)(2,1)S(1)} %get-tuple-element.191), channel_id=1, source_target_pairs={{120,0},{121,1},{122,2},{123,3},{124,4},{125,5},{126,6},{127,7},{0... | collective-permute-start | bytes 2359304 | tf_op jit(solution)/shard_map/ppermute | solution.py:14
  51.1 150.8 %collective-permute-start.7 = (bf16[384,1024]{1,0:T(8,128)(2,1)}, bf16[384,1024]{1,0:T(8,128)(2,1)}, u32[]{:S(2)}, u32[]{:S(2)}) collective-permute-start(bf16[384,1024]{1,0:T(8,128)(2,1)} %get-tuple-element.192), channel_id=1, source_target_pairs={{8,0},{9,1},{10,2},{11,3},{12,4},{13,5},{14,6},{15,7},{16,8},{17,9... | collective-permute-start | bytes 2359304 | tf_op jit(solution)/shard_map/ppermute | solution.py:14
  113.9 133.6 %collective-permute-start.3 = (bf16[384,1024]{1,0:T(8,128)(2,1)}, bf16[384,1024]{1,0:T(8,128)(2,1)}, u32[]{:S(2)}, u32[]{:S(2)}) collective-permute-start(bf16[384,1024]{1,0:T(8,128)(2,1)} %get-tuple-element.193), channel_id=1, source_target_pairs={{4,0},{5,1},{6,2},{7,3},{8,4},{9,5},{10,6},{11,7},{12,8},{13,9},{1... | collective-permute-start | bytes 2359304 | tf_op jit(solution)/shard_map/ppermute | solution.py:14
  156.7 90.8 %collective-permute-start.1 = (bf16[384,1024]{1,0:T(8,128)(2,1)}, bf16[384,1024]{1,0:T(8,128)(2,1)}, u32[]{:S(2)}, u32[]{:S(2)}) collective-permute-start(bf16[384,1024]{1,0:T(8,128)(2,1)} %get-tuple-element.194), channel_id=1, source_target_pairs={{124,0},{125,1},{126,2},{127,3},{0,4},{1,5},{2,6},{3,7},{4,8},{5,9... | collective-permute-start | bytes 2359304 | tf_op jit(solution)/shard_map/ppermute | solution.py:14
  156.7 104.3 %collective-permute-start.5 = (bf16[384,1024]{1,0:T(8,128)(2,1)}, bf16[384,1024]{1,0:T(8,128)(2,1)}, u32[]{:S(2)}, u32[]{:S(2)}) collective-permute-start(bf16[384,1024]{1,0:T(8,128)(2,1)} %get-tuple-element.195), channel_id=1, source_target_pairs={{120,0},{121,1},{122,2},{123,3},{124,4},{125,5},{126,6},{127,7},{0... | collective-permute-start | bytes 2359304 | tf_op jit(solution)/shard_map/ppermute | solution.py:14
  157.4 10.2 %copy-start.10 = (s32[1,4,6]{2,1,0:T(4,128)S(1)}, s32[1,4,6]{2,1,0:T(4,128)}, u32[]{:S(2)}) copy-start(s32[1,4,6]{2,1,0:T(4,128)} %param.19) | copy-start | bytes 292
  365.3 4.4 copy-start.6
  369.6 4.5 copy-start.3
  369.8 4.4 copy-start.8
  492.0 4.4 copy-start.6
  496.2 4.5 copy-start.3
  618.6 4.4 copy-start.6
  622.9 4.5 copy-start.3
  (14 other events, 56.0 us)
where the time goes:
time: 676 us; the launch traced here: 663 us
  local copies, waits for them, and re-layouts  321 us (47%)
  waiting for transfers between devices  183 us (27%)
  matrix products  75.3 us (11%)
  starting transfers between devices  59.3 us (9%)
  loops' own time  18.8 us (3%)
    ppermute x12, waiting for transfers between devices, passed_along(): return lax.ppermute(block, axis, route)  183 us
    concatenate x27, local copies, waits for them, and re-layouts, one_group(): jnp.concatenate(key_parts, axis=1).reshape(group_size, -1, HEADS, head_dim)  91.6 us
    concatenate x27, local copies, waits for them, and re-layouts, one_group(): jnp.concatenate(value_parts, axis=1)  86.8 us
    ppermute x12, starting transfers between devices, passed_along(): return lax.ppermute(block, axis, route)  59.3 us
    dot_general x3, matrix products, one_group(): jnp.einsum('ghqk,gkhd->gqhd', weights, value_group, preferred_element_typ...  37.1 us
    sub x3, matrix products, one_group(): expo_scores = jnp.exp(scores - row_max)  33.5 us
    gather x12, local copies, waits for them, and re-layouts, one_group(): key_tiles[source][block_index]  32.9 us
    gather x12, local copies, waits for them, and re-layouts, one_group(): value_tiles[source][block_index]  29.7 us
  transfers between devices with their start and end apart: 12, of which 6 were waited for; matrix products, arithmetic and copies ran while one was open for 2% of the time, Pallas kernels for 0%

commit v1 on v0

v1 whole, which is shorter than its diff:
```python
import functools
import math

import jax
import jax.numpy as jnp
from jax import lax
from jax.experimental import pallas as pl
from jax.experimental.pallas import tpu as pltpu
from jax.sharding import PartitionSpec as P


HEADS = 16
DEAD = 1e30


def passed_along(block, axis, distance):
    devices = range(lax.axis_size(axis))
    route = [((i - distance) % len(devices), i) for i in devices]
    return lax.ppermute(block, axis, route)


def head_masks(rows, lanes, head_dim):
    lane = lax.broadcasted_iota(jnp.int32, (rows, lanes), 1)
    return lane < head_dim


def tile_scores(q2, key_list, dead_list, mix):
    scores = []
    top = None
    for keys, dead in zip(key_list, dead_list):
        s = lax.dot_general(
            q2, keys, (((1,), (1,)), ((), ())), preferred_element_type=jnp.float32
        )
        scores.append(s)
        seen = s if dead is None else s - dead
        top = seen if top is None else jnp.maximum(top, seen)
    row_max = jnp.max(top, axis=-1, keepdims=True)
    if mix is not None:
        row_max = jnp.maximum(row_max, mix)
    return scores, row_max


def weighted(scores, row_max, dead_list, value_list, factor):
    _, block_len = scores[0].shape
    ones = jnp.ones((block_len, value_list[0].shape[1]), jnp.bfloat16)
    probs = []
    for s, dead in zip(scores, dead_list):
        level = row_max if dead is None else row_max + dead
        probs.append(jnp.exp2((s - level) * factor).astype(jnp.bfloat16))
    weights = jnp.concatenate(probs, axis=1)
    values = jnp.concatenate(
        [jnp.concatenate([v, ones], axis=1) for v in value_list], axis=0
    )
    return jnp.dot(weights, values, preferred_element_type=jnp.float32)


def near_kernel(
    factor, qblocks, block_len, head_dim,
    index_ref, dead_ref, q_ref, k_ref, v_ref, kp_ref, vp_ref, kn_ref, vn_ref,
    acc_ref, top_ref, sum_ref,
):
    pair = 2 * head_dim
    low = head_masks(block_len, pair, head_dim)

    def one_block(b, carry):
        base = pl.multiple_of(b * block_len, block_len)
        q = q_ref[pl.ds(base, block_len), :]
        zero = jnp.zeros_like(q)
        q2 = jnp.concatenate([jnp.where(low, q, zero), jnp.where(low, zero, q)], axis=0)
        keys = [k_ref[pl.ds(base, block_len), :]]
        values = [v_ref[pl.ds(base, block_len), :]]
        dead = [None]
        for source, (kr, vr) in enumerate(((kp_ref, vp_ref), (kn_ref, vn_ref))):
            for m in range(2):
                at = pl.multiple_of(index_ref[b, source * 2 + m] * block_len, block_len)
                keys.append(kr[pl.ds(at, block_len), :])
                values.append(vr[pl.ds(at, block_len), :])
                dead.append(dead_ref[b, source] if m else None)
        scores, row_max = tile_scores(q2, keys, dead, None)
        out = weighted(scores, row_max, dead, values, factor)
        top2 = jnp.broadcast_to(row_max, (2 * block_len, pair))
        acc_ref[pl.ds(base, block_len), :] = jnp.where(low, out[:block_len, :pair], out[block_len:, :pair])
        sum_ref[pl.ds(base, block_len), :] = jnp.where(low, out[:block_len, pair:], out[block_len:, pair:])
        top_ref[pl.ds(base, block_len), :] = jnp.where(low, top2[:block_len], top2[block_len:])
        return carry

    lax.fori_loop(0, qblocks, one_block, 0, unroll=True)


def far_kernel(
    factor, qblocks, block_len, head_dim, steps, first,
    index_ref, dead_ref, q_ref, kp_ref, vp_ref, kn_ref, vn_ref,
    acc_ref, top_ref, sum_ref, w_ref, base_ref, out_ref, attended_ref,
):
    pair = 2 * head_dim
    low = head_masks(block_len, pair, head_dim)
    step = pl.program_id(0)

    def one_block(b, carry):
        base = pl.multiple_of(b * block_len, block_len)
        q = q_ref[pl.ds(base, block_len), :]
        zero = jnp.zeros_like(q)
        q2 = jnp.concatenate([jnp.where(low, q, zero), jnp.where(low, zero, q)], axis=0)
        keys, values, dead = [], [], []
        for source, (kr, vr) in enumerate(((kp_ref, vp_ref), (kn_ref, vn_ref))):
            for m in range(2):
                at = pl.multiple_of(index_ref[b, source * 2 + m] * block_len, block_len)
                keys.append(kr[pl.ds(at, block_len), :])
                values.append(vr[pl.ds(at, block_len), :])
                dead.append(dead_ref[b, source] if m else None)
        top = top_ref[pl.ds(base, block_len), :]
        start = jnp.concatenate([top[:, :1], top[:, head_dim:head_dim + 1]], axis=0)
        scores, row_max = tile_scores(q2, keys, dead, start)
        out = weighted(scores, row_max, dead, values, factor)
        top2 = jnp.broadcast_to(row_max, (2 * block_len, pair))
        now = jnp.where(low, top2[:block_len], top2[block_len:])
        fade = jnp.exp2((top - now) * factor)
        acc = acc_ref[pl.ds(base, block_len), :] * fade + jnp.where(
            low, out[:block_len, :pair], out[block_len:, :pair])
        total = sum_ref[pl.ds(base, block_len), :] * fade + jnp.where(
            low, out[:block_len, pair:], out[block_len:, pair:])
        attended_ref[step, pl.ds(base, block_len), :] = (acc / total).astype(jnp.bfloat16)
        return carry

    lax.fori_loop(0, qblocks, one_block, 0, unroll=True)

    @pl.when(step == steps - 1)
    def _():
        def project(b, carry):
            base = pl.multiple_of(b * block_len, block_len)
            rows = jnp.concatenate(
                [attended_ref[i, pl.ds(base, block_len), :] for i in range(steps)], axis=1
            )
            out_ref[pl.ds(base, block_len), :] = (
                base_ref[pl.ds(base, block_len), :].astype(jnp.float32)
                + jnp.dot(rows, w_ref[first:first + steps * pair, :], preferred_element_type=jnp.float32)
            ).astype(out_ref.dtype)
            return carry

        lax.fori_loop(0, qblocks, project, 0)


def attend_near(index, dead, q, k, v, kp, vp, kn, vn, qblocks, head_dim):
    tokens, width = q.shape
    block_len = tokens // qblocks
    pair = 2 * head_dim
    factor = math.log2(math.e) / math.sqrt(head_dim)
    column = lambda g, *_: (0, g)
    spec = pl.BlockSpec((tokens, pair), column)
    shape = jax.ShapeDtypeStruct((tokens, width), jnp.float32)
    keys_seen = 5 * block_len
    return pl.pallas_call(
        functools.partial(near_kernel, factor, qblocks, block_len, head_dim),
        grid_spec=pltpu.PrefetchScalarGridSpec(
            num_scalar_prefetch=2,
            grid=(width // pair,),
            in_specs=[spec] * 7,
            out_specs=[spec] * 3,
        ),
        out_shape=[shape] * 3,
        name="near",
        cost_estimate=pl.CostEstimate(
            flops=8 * tokens * keys_seen * width, bytes_accessed=7 * tokens * width * 2 + 12 * tokens * width,
            transcendentals=tokens * keys_seen * (width // head_dim)),
        compiler_params=pltpu.CompilerParams(vmem_limit_bytes=40 * 2**20),
    )(index, dead, q, k, v, kp, vp, kn, vn)


def attend_far(
    index, dead, q, kp, vp, kn, vn, acc, top, total, w, base, first, out_dtype, qblocks, head_dim
):
    tokens, width = q.shape
    block_len = tokens // qblocks
    pair = 2 * head_dim
    chunk = vp.shape[1]
    steps = chunk // pair
    factor = math.log2(math.e) / math.sqrt(head_dim)
    offset = first // pair
    shifted = lambda g, *_: (0, g + offset)
    local = lambda g, *_: (0, g)
    whole = lambda g, *_: (0, 0)
    window = vp.shape[0]
    carry = pl.BlockSpec((tokens, pair), shifted)
    keys_seen = 4 * block_len
    return pl.pallas_call(
        functools.partial(
            far_kernel, factor, qblocks, block_len, head_dim, steps, first),
        grid_spec=pltpu.PrefetchScalarGridSpec(
            num_scalar_prefetch=2,
            grid=(steps,),
            in_specs=[
                carry,
                pl.BlockSpec((window, pair), shifted),
                pl.BlockSpec((window, pair), local),
                pl.BlockSpec((window, pair), shifted),
                pl.BlockSpec((window, pair), local),
                carry, carry, carry,
                pl.BlockSpec((width, width), whole),
                pl.BlockSpec((tokens, width), whole),
            ],
            out_specs=pl.BlockSpec((tokens, width), whole),
            scratch_shapes=[pltpu.VMEM((steps, tokens, pair), jnp.bfloat16)],
        ),
        out_shape=jax.ShapeDtypeStruct((tokens, width), out_dtype),
        name="far",
        cost_estimate=pl.CostEstimate(
            flops=8 * tokens * keys_seen * chunk + 2 * tokens * chunk * width,
            bytes_accessed=14 * tokens * chunk + 10 * tokens * width,
            transcendentals=tokens * keys_seen * (chunk // head_dim)),
        compiler_params=pltpu.CompilerParams(vmem_limit_bytes=40 * 2**20),
    )(index, dead, q, kp, vp, kn, vn, acc, top, total, w, base)


def per_device(
    queries, keys, values, residual, w_out, neighbours, band_start, band_blocks, band_count
):
    q, k, v = queries[0], keys[0], values[0]
    tokens, width = q.shape
    qblocks = band_count.shape[2]
    block_len = tokens // qblocks
    window = max(2, qblocks // 2) * block_len
    head_dim = width // HEADS
    cameras = lax.axis_size("cam")
    rigs = cameras // min(32, cameras)
    me = lax.axis_index("cam")
    offsets = (1, -1, 2, -2)
    pair = 2 * head_dim
    early = (width // pair * 5 // 8) * pair
    chunks = ((0, early), (early, width - early))

    k_prev = passed_along(k, "cam", rigs)
    k_next = passed_along(k, "cam", -rigs)
    v_prev = passed_along(v, "cam", rigs)
    v_next = passed_along(v, "cam", -rigs)

    sources = jnp.stack([(me - offset * rigs + 2 * cameras) % cameras for offset in offsets])
    match = (neighbours[0][None, :] == sources[:, None]).astype(jnp.int32)
    starts = jnp.sum(match * band_start[0][None, :], axis=1)
    blocks = jnp.sum(match[:, :, None, None] * band_blocks[0][None], axis=1)
    counts = jnp.sum(match[:, :, None] * band_count[0][None], axis=1)
    live = jnp.arange(2, dtype=jnp.int32)[None, None, :] < counts[:, :, None]
    blocks = jnp.where(live, blocks, blocks[:, :, :1])
    near_blocks = blocks[:2] + starts[:2, None, None]
    as_table = lambda t: jnp.transpose(t, (1, 0, 2)).reshape(qblocks, 4)
    near_index, far_index = as_table(near_blocks), as_table(blocks[2:])
    dead = jnp.where(counts > 1, 0.0, DEAD).astype(jnp.float32)
    near_dead, far_dead = dead[:2].T, dead[2:].T

    ask_prev = passed_along(lax.slice_in_dim(starts, 2, 3), "cam", -rigs)[0]
    ask_next = passed_along(lax.slice_in_dim(starts, 3, 4), "cam", rigs)[0]

    def cut(rows, start, first, size):
        return lax.dynamic_slice(rows, (start * block_len, first), (window, size))

    far_k_prev = passed_along(cut(k_prev, ask_prev, 0, width), "cam", rigs)
    far_k_next = passed_along(cut(k_next, ask_next, 0, width), "cam", -rigs)
    far_v = []
    for (first, size) in chunks:
        far_v.append((
            passed_along(cut(v_prev, ask_prev, first, size), "cam", rigs),
            passed_along(cut(v_next, ask_next, first, size), "cam", -rigs),
        ))

    acc, top, total = attend_near(
        near_index, near_dead, q, k, v, k_prev, v_prev, k_next, v_next, qblocks, head_dim)
    result = residual[0]
    for (first, size), (far_v_prev, far_v_next) in zip(chunks, far_v):
        result = attend_far(
            far_index, far_dead, q, far_k_prev, far_v_prev, far_k_next, far_v_next,
            acc, top, total, w_out, result, first,
            jnp.bfloat16 if first + size == width else jnp.float32, qblocks, head_dim)
    return result[None]


def solution(mesh):
    return jax.shard_map(
        per_device,
        mesh=mesh,
        in_specs=(
            P(("scene", "cam"), None, None),
            P(("scene", "cam"), None, None),
            P(("scene", "cam"), None, None),
            P(("scene", "cam"), None, None),
            P(),
            P(("scene", "cam"), None),
            P(("scene", "cam"), None),
            P(("scene", "cam"), None, None, None),
            P(("scene", "cam"), None, None),
        ),
        out_specs=P(("scene", "cam"), None, None),
        check_vma=False,
    )
```

time: 676 us -> 291 us (0.43); the launches traced: 663 us -> 291 us
  local copies, waits for them, and re-layouts: 321 us -> 15.4 us
  matrix products: 75.3 us -> 0 us
  Pallas kernels: 0 us -> 48.5 us
  loops' own time: 18.8 us -> 0 us
  starting transfers between devices: 59.3 us -> 43.7 us
    concatenate x57 -> x0, local copies, waits for them, and re-layouts: 178 us -> none  [the longest x27 91.6 us: one_group(): jnp.concatenate(key_parts, axis=1).reshape(group_size, -1, HEADS, head_dim)]
    gather x24 -> x0, local copies, waits for them, and re-layouts: 62.7 us -> none  [the longest x12 32.9 us: one_group(): key_tiles[source][block_index]]
    pallas_call x0 -> x3, Pallas kernels: none -> 48.5 us  [the longest x2 27 us: attend_far(): pl.pallas_call(functools.partial(far_kernel, factor, qblocks, block_len,...]
    dot_general x4 -> x0, matrix products: 41.9 us -> none  [the longest x3 37.1 us: one_group(): jnp.einsum('ghqk,gkhd->gqhd', weights, value_group, preferred_element_typ...]
    sub x3 -> x0, matrix products: 33.5 us -> none  [one_group(): expo_scores = jnp.exp(scores - row_max)]
    while x92 -> x0, local copies, waits for them, and re-layouts: 31.9 us -> none
    another operation x1 -> x0, loops' own time: 18.8 us -> none  [per_device(): lax.map(one_group, jnp.arange(group_count, dtype=jnp.int32))]
    dynamic_slice x15 -> x6, local copies, waits for them, and re-layouts: 25.5 us -> 8.82 us  [cut(): return lax.dynamic_slice(rows, (start * block_len, first), (window, size))]
  transfers between devices with their start and end apart: 12 -> 12, of which waited for: 6 -> 3; matrix products, arithmetic and copies ran while one was open for 2% -> 4% of each run, Pallas kernels for 0% -> 12%
where the time goes in v1:
time: 291 us
  waiting for transfers between devices  179 us (62%)
  Pallas kernels  48.5 us (17%)
  starting transfers between devices  43.7 us (15%)
  local copies, waits for them, and re-layouts  15.4 us (5%)
    ppermute x12, waiting for transfers between devices, passed_along(): return lax.ppermute(block, axis, route)  179 us
    ppermute x12, starting transfers between devices, passed_along(): return lax.ppermute(block, axis, route)  43.7 us
    pallas_call x2, Pallas kernels, attend_far(): pl.pallas_call(functools.partial(far_kernel, factor, qblocks, block_len,...  27 us
    pallas_call x1, Pallas kernels, attend_near(): pl.pallas_call(functools.partial(near_kernel, factor, qblocks, block_len,...  21.5 us
    dynamic_slice x6, local copies, waits for them, and re-layouts, cut(): return lax.dynamic_slice(rows, (start * block_len, first), (window, size))  8.82 us
  transfers between devices with their start and end apart: 12, of which 3 were waited for; matrix products, arithmetic and copies ran while one was open for 4% of the time, Pallas kernels for 12%

profile of v1, /device:TPU:40, one launch (start us, length us, event | category | flops | bytes accessed | tf_op | source)
XLA Modules:
  0.0 290.9 jit_solution(15258057415262069750)
XLA Ops:
  0.0 5.0 %collective-permute-start = (bf16[768,1024]{1,0:T(8,128)(2,1)}, bf16[768,1024]{1,0:T(8,128)(2,1)S(1)}, u32[]{:S(2)}, u32[]{:S(2)}) collective-permute-start(bf16[768,1024]{1,0:T(8,128)(2,1)} %bitcast.33), channel_id=1, source_target_pairs={{124,0},{125,1},{126,2},{127,3},{0,4},{1,5},{2,6},{3,7},{4,8},{5,9... | collective-permute-start | bytes 4718600 | tf_op jit(solution)/shard_map/ppermute | solution.py:19
  5.0 19.6 %collective-permute-start.5 = (bf16[768,1024]{1,0:T(8,128)(2,1)}, bf16[768,1024]{1,0:T(8,128)(2,1)}, u32[]{:S(2)}, u32[]{:S(2)}) collective-permute-start(bf16[768,1024]{1,0:T(8,128)(2,1)} %bitcast.34), channel_id=1, source_target_pairs={{4,0},{5,1},{6,2},{7,3},{8,4},{9,5},{10,6},{11,7},{12,8},{13,9},{1... | collective-permute-start | bytes 4718600 | tf_op jit(solution)/shard_map/ppermute | solution.py:19
  24.6 6.2 %collective-permute-start.8 = (bf16[768,1024]{1,0:T(8,128)(2,1)}, bf16[768,1024]{1,0:T(8,128)(2,1)}, u32[]{:S(2)}, u32[]{:S(2)}) collective-permute-start(bf16[768,1024]{1,0:T(8,128)(2,1)} %bitcast.37), channel_id=1, source_target_pairs={{4,0},{5,1},{6,2},{7,3},{8,4},{9,5},{10,6},{11,7},{12,8},{13,9},{1... | collective-permute-start | bytes 4718600 | tf_op jit(solution)/shard_map/ppermute | solution.py:19
  30.9 0.9 fusion
  32.3 0.7 copy.22
  33.0 0.7 compare_convert_fusion
  33.9 0.8 multiply_reduce_fusion.1
  34.8 125.4 %collective-permute-done.1 = s32[1]{0:T(128)} collective-permute-done((s32[1]{0:T(128)}, s32[1]{0:T(128)}, u32[]{:S(2)}, u32[]{:S(2)}) %collective-permute-start.1) | collective-permute-done | bytes 36 | tf_op jit(solution)/shard_map/ppermute | solution.py:19
  160.9 7.8 %collective-permute-done.6 = s32[1]{0:T(128)} collective-permute-done((s32[1]{0:T(128)}, s32[1]{0:T(128)}, u32[]{:S(2)}, u32[]{:S(2)}) %collective-permute-start.6) | collective-permute-done | bytes 36 | tf_op jit(solution)/shard_map/ppermute | solution.py:19
  169.4 1.0 constant_dynamic-slice_fusion.3
  170.8 2.1 constant_dynamic-slice_fusion.2
  172.9 5.9 %collective-permute-start.7 = (bf16[384,1024]{1,0:T(8,128)(2,1)}, bf16[384,1024]{1,0:T(8,128)(2,1)S(1)}, u32[]{:S(2)}, u32[]{:S(2)}) collective-permute-start(bf16[384,1024]{1,0:T(8,128)(2,1)} %constant_dynamic-slice_fusion.2), channel_id=1, source_target_pairs={{4,0},{5,1},{6,2},{7,3},{8,4},{9,5},{10,6},{11,7},{12,8},{13,9},{1... | collective-permute-start | bytes 2359304 | tf_op jit(solution)/shard_map/ppermute | solution.py:19
  178.7 1.9 constant_dynamic-slice_fusion.1
  180.8 1.1 constant_dynamic-slice_fusion.5
  182.1 1.1 constant_dynamic-slice_fusion
  183.2 6.4 %collective-permute-start.11 = (bf16[384,640]{1,0:T(8,128)(2,1)S(1)}, bf16[384,640]{1,0:T(8,128)(2,1)S(1)}, u32[]{:S(2)}, u32[]{:S(2)}) collective-permute-start(bf16[384,640]{1,0:T(8,128)(2,1)S(1)} %constant_dynamic-slice_fusion), channel_id=1, source_target_pairs={{4,0},{5,1},{6,2},{7,3},{8,4},{9,5},{10,6},{11,7},{12,8},{13,9},{1... | collective-permute-start | bytes 1474568 | tf_op jit(solution)/shard_map/ppermute | solution.py:19
  189.5 1.7 constant_dynamic-slice_fusion.4
  191.3 46.1 %collective-permute-done.10.vp_ref = bf16[384,640]{1,0:T(8,128)(2,1)} collective-permute-done((bf16[384,640]{1,0:T(8,128)(2,1)}, bf16[384,640]{1,0:T(8,128)(2,1)}, u32[]{:S(2)}, u32[]{:S(2)}) %collective-permute-start.10) | collective-permute-done | bytes 491552 | tf_op jit(solution)/shard_map/ppermute | solution.py:19
  237.8 1.4 copy-done.7
  239.2 1.4 copy-done.8
  240.7 21.5 %near.1 = (f32[768,1024]{1,0:T(8,128)S(1)}, f32[768,1024]{1,0:T(8,128)}, f32[768,1024]{1,0:T(8,128)}) custom-call(s32[6,4]{1,0:T(8,128)S(1)} %copy.18.index_ref, f32[6,2]{1,0:T(8,128)S(1)} %get-tuple-element.11.dead_ref, bf16[768,1024]{1,0:T(8,128)(2,1)S(1)} %bitcast.29, bf16[768,1024]{1,0:T(8,128)(2,1)S(1)} %bitcast.35, bf16[768,1024]{1,0:T(8,128)(2,1)S(1)} %bitcast.38, ...), custom_call_target="tpu_custom_call" | custom-call | flops 4026531840 | bytes 20447232 | tf_op jit(solution)/shard_map/near/pallas_call | solution.py:152
  262.2 14.8 %far.2.base_ref = f32[768,1024]{1,0:T(8,128)S(1)} custom-call(s32[6,4]{1,0:T(8,128)S(1)} %copy.20.index_ref, f32[6,2]{1,0:T(8,128)S(1)} %get-tuple-element.12.dead_ref, bf16[768,1024]{1,0:T(8,128)(2,1)S(1)} %bitcast.30, bf16[384,1024]{1,0:T(8,128)(2,1)S(1)} %collective-permute-done.2.kp_ref, bf16[384,640]{1,0:T(8,128)(2,1)} %collective-permute-done.10.vp_ref, ...), custom_call_target="tpu_custom_call" | custom-call | flops 3019898880 | bytes 14745600 | tf_op jit(solution)/shard_map/far/pallas_call | solution.py:185
  277.0 1.7 copy-done.1
  278.7 12.2 %far.3 = bf16[768,1024]{1,0:T(8,128)(2,1)} custom-call(s32[6,4]{1,0:T(8,128)S(1)} %copy.20.index_ref, f32[6,2]{1,0:T(8,128)S(1)} %get-tuple-element.12.dead_ref, bf16[768,1024]{1,0:T(8,128)(2,1)S(1)} %bitcast.31, bf16[384,1024]{1,0:T(8,128)(2,1)S(1)} %collective-permute-done.2.kp_ref, bf16[384,384]{1,0:T(8,128)(2,1)S(1)} %collective-permute-done.4.vp_ref, ...), custom_call_target="tpu_custom_call" | custom-call | flops 1811939328 | bytes 11993088 | tf_op jit(solution)/shard_map/far/pallas_call | solution.py:185
  (42 shorter events, 2.3 us)
Async XLA Ops:
  0.0 169.4 %collective-permute-start = (bf16[768,1024]{1,0:T(8,128)(2,1)}, bf16[768,1024]{1,0:T(8,128)(2,1)S(1)}, u32[]{:S(2)}, u32[]{:S(2)}) collective-permute-start(bf16[768,1024]{1,0:T(8,128)(2,1)} %bitcast.33), channel_id=1, source_target_pairs={{124,0},{125,1},{126,2},{127,3},{0,4},{1,5},{2,6},{3,7},{4,8},{5,9... | collective-permute-start | bytes 4718600 | tf_op jit(solution)/shard_map/ppermute | solution.py:19
  5.0 165.4 %collective-permute-start.5 = (bf16[768,1024]{1,0:T(8,128)(2,1)}, bf16[768,1024]{1,0:T(8,128)(2,1)}, u32[]{:S(2)}, u32[]{:S(2)}) collective-permute-start(bf16[768,1024]{1,0:T(8,128)(2,1)} %bitcast.34), channel_id=1, source_target_pairs={{4,0},{5,1},{6,2},{7,3},{8,4},{9,5},{10,6},{11,7},{12,8},{13,9},{1... | collective-permute-start | bytes 4718600 | tf_op jit(solution)/shard_map/ppermute | solution.py:19
  24.6 154.2 %collective-permute-start.3 = (bf16[768,1024]{1,0:T(8,128)(2,1)}, bf16[768,1024]{1,0:T(8,128)(2,1)}, u32[]{:S(2)}, u32[]{:S(2)}) collective-permute-start(bf16[768,1024]{1,0:T(8,128)(2,1)} %bitcast.36), channel_id=1, source_target_pairs={{124,0},{125,1},{126,2},{127,3},{0,4},{1,5},{2,6},{3,7},{4,8},{5,9... | collective-permute-start | bytes 4718600 | tf_op jit(solution)/shard_map/ppermute | solution.py:19
  24.6 157.5 %collective-permute-start.8 = (bf16[768,1024]{1,0:T(8,128)(2,1)}, bf16[768,1024]{1,0:T(8,128)(2,1)}, u32[]{:S(2)}, u32[]{:S(2)}) collective-permute-start(bf16[768,1024]{1,0:T(8,128)(2,1)} %bitcast.37), channel_id=1, source_target_pairs={{4,0},{5,1},{6,2},{7,3},{8,4},{9,5},{10,6},{11,7},{12,8},{13,9},{1... | collective-permute-start | bytes 4718600 | tf_op jit(solution)/shard_map/ppermute | solution.py:19
  32.3 127.9 %collective-permute-start.1 = (s32[1]{0:T(128)}, s32[1]{0:T(128)}, u32[]{:S(2)}, u32[]{:S(2)}) collective-permute-start(s32[1]{0:T(128)} %get-tuple-element.16), channel_id=1, source_target_pairs={{4,0},{5,1},{6,2},{7,3},{8,4},{9,5},{10,6},{11,7},{12,8},{13,9},{1... | collective-permute-start | bytes 20 | tf_op jit(solution)/shard_map/ppermute | solution.py:19
  160.3 8.4 %collective-permute-start.6 = (s32[1]{0:T(128)}, s32[1]{0:T(128)}, u32[]{:S(2)}, u32[]{:S(2)}) collective-permute-start(s32[1]{0:T(128)} %get-tuple-element.15), channel_id=1, source_target_pairs={{124,0},{125,1},{126,2},{127,3},{0,4},{1,5},{2,6},{3,7},{4,8},{5,9... | collective-permute-start | bytes 20 | tf_op jit(solution)/shard_map/ppermute | solution.py:19
  169.4 1.4 copy-start.5
  170.4 91.8 %collective-permute-start.2 = (bf16[384,1024]{1,0:T(8,128)(2,1)}, bf16[384,1024]{1,0:T(8,128)(2,1)S(1)}, u32[]{:S(2)}, u32[]{:S(2)}) collective-permute-start(bf16[384,1024]{1,0:T(8,128)(2,1)} %constant_dynamic-slice_fusion.3), channel_id=1, source_target_pairs={{124,0},{125,1},{126,2},{127,3},{0,4},{1,5},{2,6},{3,7},{4,8},{5,9... | collective-permute-start | bytes 2359304 | tf_op jit(solution)/shard_map/ppermute | solution.py:19
  172.9 65.0 %copy-start.3 = (bf16[1,768,1024]{2,1,0:T(8,128)(2,1)S(1)}, bf16[1,768,1024]{2,1,0:T(8,128)(2,1)}, u32[]{:S(2)}) copy-start(bf16[1,768,1024]{2,1,0:T(8,128)(2,1)} %param.9) | copy-start | bytes 4718596
  172.9 89.3 %collective-permute-start.7 = (bf16[384,1024]{1,0:T(8,128)(2,1)}, bf16[384,1024]{1,0:T(8,128)(2,1)S(1)}, u32[]{:S(2)}, u32[]{:S(2)}) collective-permute-start(bf16[384,1024]{1,0:T(8,128)(2,1)} %constant_dynamic-slice_fusion.2), channel_id=1, source_target_pairs={{4,0},{5,1},{6,2},{7,3},{8,4},{9,5},{10,6},{11,7},{12,8},{13,9},{1... | collective-permute-start | bytes 2359304 | tf_op jit(solution)/shard_map/ppermute | solution.py:19
  180.6 56.7 %collective-permute-start.10 = (bf16[384,640]{1,0:T(8,128)(2,1)}, bf16[384,640]{1,0:T(8,128)(2,1)}, u32[]{:S(2)}, u32[]{:S(2)}) collective-permute-start(bf16[384,640]{1,0:T(8,128)(2,1)} %constant_dynamic-slice_fusion.1), channel_id=1, source_target_pairs={{124,0},{125,1},{126,2},{127,3},{0,4},{1,5},{2,6},{3,7},{4,8},{5,9... | collective-permute-start | bytes 1474568 | tf_op jit(solution)/shard_map/ppermute | solution.py:19
  180.8 57.0 %copy-start.6 = (bf16[768,1024]{1,0:T(8,128)(2,1)S(1)}, bf16[768,1024]{1,0:T(8,128)(2,1)}, u32[]{:S(2)}) copy-start(bf16[768,1024]{1,0:T(8,128)(2,1)} %copy-done.5) | copy-start | bytes 4718596
  182.0 96.8 %collective-permute-start.4 = (bf16[384,384]{1,0:T(8,128)(2,1)S(1)}, bf16[384,384]{1,0:T(8,128)(2,1)S(1)}, u32[]{:S(2)}, u32[]{:S(2)}) collective-permute-start(bf16[384,384]{1,0:T(8,128)(2,1)S(1)} %constant_dynamic-slice_fusion.5), channel_id=1, source_target_pairs={{124,0},{125,1},{126,2},{127,3},{0,4},{1,5},{2,6},{3,7},{4,8},{5,9... | collective-permute-start | bytes 884744 | tf_op jit(solution)/shard_map/ppermute | solution.py:19
  183.2 79.0 %collective-permute-start.11 = (bf16[384,640]{1,0:T(8,128)(2,1)S(1)}, bf16[384,640]{1,0:T(8,128)(2,1)S(1)}, u32[]{:S(2)}, u32[]{:S(2)}) collective-permute-start(bf16[384,640]{1,0:T(8,128)(2,1)S(1)} %constant_dynamic-slice_fusion), channel_id=1, source_target_pairs={{4,0},{5,1},{6,2},{7,3},{8,4},{9,5},{10,6},{11,7},{12,8},{13,9},{1... | collective-permute-start | bytes 1474568 | tf_op jit(solution)/shard_map/ppermute | solution.py:19
  237.3 41.4 %collective-permute-start.9 = (bf16[384,384]{1,0:T(8,128)(2,1)}, bf16[384,384]{1,0:T(8,128)(2,1)S(1)}, u32[]{:S(2)}, u32[]{:S(2)}) collective-permute-start(bf16[384,384]{1,0:T(8,128)(2,1)} %constant_dynamic-slice_fusion.4), channel_id=1, source_target_pairs={{4,0},{5,1},{6,2},{7,3},{8,4},{9,5},{10,6},{11,7},{12,8},{13,9},{1... | collective-permute-start | bytes 884744 | tf_op jit(solution)/shard_map/ppermute | solution.py:19
  237.8 1.4 copy-start.7
  239.2 1.4 copy-start.8
  240.7 21.6 %copy-start.2 = (bf16[1024,1024]{1,0:T(8,128)(2,1)S(1)}, bf16[1024,1024]{1,0:T(8,128)(2,1)}, u32[]{:S(2)}) copy-start(bf16[1024,1024]{1,0:T(8,128)(2,1)} %w_ref.3) | copy-start | bytes 6291460
  240.7 21.6 %copy-start.4 = (bf16[1,768,1024]{2,1,0:T(8,128)(2,1)S(1)}, bf16[1,768,1024]{2,1,0:T(8,128)(2,1)}, u32[]{:S(2)}) copy-start(bf16[1,768,1024]{2,1,0:T(8,128)(2,1)} %param.12) | copy-start | bytes 4718596
  262.2 16.5 %copy-start = (f32[768,1024]{1,0:T(8,128)S(1)}, f32[768,1024]{1,0:T(8,128)}, u32[]{:S(2)}) copy-start(f32[768,1024]{1,0:T(8,128)} %get-tuple-element.9.top_ref) | copy-start | bytes 9437188
  277.0 1.7 copy-start.1
